TPU v7x, 512 devices: a 8x2x16 block of a 8x16x16 slice. The times are simulated.
512 devices in a mesh: ckpt: 2 (over y), row: 32 (over z, core), col: 8 (over x).
Axes of the slice: x: 8, y: 2, z: 16, core: 2. Of those that a mesh axis runs over, the one named last changes fastest.
The devices are a block of a 8x16x16 slice.
Arguments:
- grad_slab: bfloat16 [768, 27648], P(('ckpt', 'col'), 'row'), parts along dimension 0, may hold values from -6 to 6
- eigenbasis: bfloat16 [55296, 14336], P(('ckpt', 'row'), 'col'), parts along dimension 0, may hold values from -0.0625 to 0.0625
- eigenvalues: bfloat16 [768, 14336], P('ckpt', 'col'), parts along dimension 0, may hold values from 0.049804688 to 5
Outputs:
- preconditioned: bfloat16 [768, 27648], P(('ckpt', 'col'), 'row'), parts along dimension 0
There are 2 independent parts, one for each index of `ckpt`. A program takes and returns all parts, laid end to end along the dimension named above; each array names one. Nothing has to cross between parts.
All inputs are finite; a program needn't handle non-finite values.
Results may differ from a plain program's by a relative error of at most 0.0046.
Values may be sent and summed in bfloat16 or wider, within the bound.
A program may use at most 64 MiB of HBM per device.

v0:
```python
import jax
import jax.numpy as jnp
from jax import lax
from jax.sharding import Mesh
from jax.sharding import PartitionSpec as P

ROW = ("row_0", "row_1")
CKPT_ROW = ("ckpt", "row_0", "row_1")
DAMPING = 0.1


def laid_out(blocks, dim):
    blocks = jnp.moveaxis(blocks, 0, dim)
    lengths = blocks.shape
    return blocks.reshape(*lengths[:dim], lengths[dim] * lengths[dim + 1], *lengths[dim + 2 :])


def copy_for_each(value, axis):
    copies = jnp.broadcast_to(value, (lax.axis_size(axis), *value.shape))
    return lax.all_to_all(copies, axis, split_axis=0, concat_axis=0, tiled=True)


def gather_directly(value, axis, dim):
    return laid_out(copy_for_each(value, axis), dim)


def reduced_to_own(blocks, axes, order):
    inside = blocks.shape[1:]
    blocks = blocks.reshape(*(lax.axis_size(a) for a in axes), *inside)
    blocks = jnp.moveaxis(blocks, order, range(len(axes))).reshape(-1, *inside)
    for k in order:
        blocks = lax.psum_scatter(blocks, axes[k], scatter_dimension=0, tiled=True)
    return blocks[0]


def split_up(value, dim, count):
    before, after = (value.shape[:dim], value.shape[dim + 1 :])
    return jnp.moveaxis(value.reshape(*before, count, -1, *after), dim, 0)


def scatter_axes(value, axes, order, dim):
    count = lax.axis_size(axes)
    return reduced_to_own(split_up(value, dim, count), axes, order)


def all_blocks(value, axes, order):
    blocks = value[None]
    for k in order:
        blocks = lax.all_gather(blocks, axes[k], axis=0, tiled=True)
    carried = [lax.axis_size(axes[k]) for k in reversed(order)]
    blocks = blocks.reshape(*carried, *value.shape)
    turned = sorted(range(len(order)), key=lambda place: order[len(order) - 1 - place])
    return blocks.transpose(*turned, *range(len(order), blocks.ndim)).reshape(-1, *value.shape)


def whole_of(value, axes, order, dim):
    return laid_out(all_blocks(value, axes, order), dim)


def summed_on_arrival(value, axis, dim):
    count = lax.axis_size(axis)
    blocks = lax.all_to_all(split_up(value, dim, count), axis, 0, 0, tiled=True)
    return jnp.sum(blocks, axis=0)


def on_device(grad_slab, eigenbasis, eigenvalues):
    rotated_part = jnp.dot(
        gather_directly(grad_slab, "col", 0), eigenbasis, preferred_element_type=jnp.float32
    )
    own_share = scatter_axes(rotated_part, ROW, (1, 0), 1)
    share_width = own_share.shape[1]
    offset = lax.axis_index(ROW) * share_width
    own_values = lax.dynamic_slice_in_dim(eigenvalues, offset, share_width, 1)
    scaled_share = (own_share / (own_values.astype(jnp.float32) + DAMPING)).astype(jnp.bfloat16)
    scaled = whole_of(scaled_share, ROW, (0, 1), 1)
    result = summed_on_arrival(
        lax.dot_general(
            scaled, eigenbasis, (((1,), (1,)), ((), ())), preferred_element_type=jnp.float32
        ),
        "col",
        0,
    )
    return result.astype(jnp.bfloat16)


def solution(mesh):
    torus = Mesh(
        mesh.devices.reshape(mesh.shape["ckpt"], 16, 2, mesh.shape["col"]),
        ("ckpt", "row_0", "row_1", "col"),
    )
    return jax.shard_map(
        on_device,
        mesh=torus,
        in_specs=(P(("ckpt", "col"), ROW), P(CKPT_ROW, "col"), P("ckpt", "col")),
        out_specs=P(("ckpt", "col"), ROW),
        check_vma=False,
    )
```

profile of v0, /device:TPU:65, one launch (start us, length us, event | category | flops | bytes accessed | tf_op | source)
XLA Modules:
  0.0 314.1 jit_solution(3465347139622952609)
XLA Ops:
  6.5 1.8 broadcast_in_dim.6
  8.3 7.9 %all-to-all-start = ((bf16[8,48,864]{2,1,0:T(8,128)(2,1)}), bf16[8,48,864]{2,1,0:T(8,128)(2,1)}, u32[]{:S(2)}, u32[]{:S(2)}) async-start(bf16[8,48,864]{2,1,0:T(8,128)(2,1)} %broadcast_in_dim.6), calls=%async_computation | async-start | bytes 1376256 | tf_op jit(solution)/shard_map/all_to_all | solution.py:20
  16.2 0.1 reduce-scatter.3.cloned.1.call-start
  16.3 4.5 %copy.16 = bf16[864,1792]{0,1:T(8,128)(2,1)S(1)} copy(bf16[864,1792]{1,0:T(8,128)(2,1)} %param.4) | data formatting | bytes 6193152 | tf_op args[1]
  20.8 9.4 %all-to-all-done = bf16[8,48,864]{2,1,0:T(8,128)(2,1)} async-done(((bf16[8,48,864]{2,1,0:T(8,128)(2,1)}), bf16[8,48,864]{2,1,0:T(8,128)(2,1)}, u32[]{:S(2)}, u32[]{:S(2)}) %all-to-all-start) | async-done | bytes 663584 | tf_op jit(solution)/shard_map/all_to_all | solution.py:20
  30.2 4.8 %fusion.3 = f32[384,32,56]{0,2,1:T(8,128)} fusion(bf16[384,864,1]{1,0,2:T(8,128)(2,1)} %bitcast.1, bf16[32,56,864]{2,1,0:T(8,128)(2,1)S(1)} %bitcast.32), kind=kOutput, calls=%fused_computation.4 | convolution fusion | flops 1189085184 | bytes 6512640 | tf_op jit(solution)/shard_map/dot_general | solution.py:67
  35.1 5.6 %copy.18 = f32[2,16,384,56]{3,2,1,0:T(8,128)} copy(f32[2,16,384,56]{2,3,0,1:T(8,128)} %bitcast.33) | data formatting | bytes 5505024 | tf_op jit(solution)/shard_map/transpose | solution.py:30
  40.7 0.1 reduce-scatter.3.cloned.1.call-update
  40.7 0.1 reduce-scatter.5.cloned.1.call-start
  40.8 64.1 %reduce-scatter.3.cloned.1.call-done = f32[16,384,56]{2,1,0:T(8,128)} async-done(((f32[32,384,56]{2,1,0:T(8,128)}), f32[16,384,56]{2,1,0:T(8,128)}) %reduce-scatter.3.cloned.1.call-update) | async-done | bytes 1376272 | tf_op jit(solution)/shard_map/reduce_scatter | solution.py:32
  104.9 0.1 reduce-scatter.5.cloned.1.call-update
  104.9 0.1 all-gather.3.cloned.1.call-start
  105.0 73.0 %reduce-scatter.5.cloned.1.call-done = f32[1,384,56]{2,1,0:T(8,128)} async-done(((f32[16,384,56]{2,1,0:T(8,128)}), f32[1,384,56]{2,1,0:T(8,128)}) %reduce-scatter.5.cloned.1.call-update) | async-done | bytes 86032 | tf_op jit(solution)/shard_map/reduce_scatter | solution.py:32
  178.0 1.1 fusion.2
  179.1 30.7 %all-gather = bf16[6144,56]{1,0:T(8,128)(2,1)S(1)} all-gather(bf16[384,56]{1,0:T(8,128)(2,1)S(1)} %fusion.2), channel_id=2, replica_groups=mesh['ckpt'=2,'row_0'=16,'row_1'=2,'col'=8] {'row_0'}, dimensions={0}, use_global_device_ids=true | all-gather | bytes 731136 | tf_op jit(solution)/shard_map/all_gather | solution.py:49
  209.8 1.4 copy.20
  211.2 0.1 all-gather.3.cloned.1.call-update
  211.3 38.6 %all-gather.3.cloned.1.call-done = bf16[32,384,56]{1,2,0:T(8,128)(2,1)} async-done(((bf16[16,384,56]{1,2,0:T(8,128)(2,1)}), bf16[32,384,56]{1,2,0:T(8,128)(2,1)}) %all-gather.3.cloned.1.call-update) | async-done | bytes 1376272 | tf_op jit(solution)/shard_map/all_gather | solution.py:49
  249.9 7.0 %copy.21 = bf16[16,2,384,56]{3,1,0,2:T(2,128)(2,1)S(1)} copy(bf16[16,2,384,56]{2,3,0,1:T(8,128)(2,1)} %bitcast.34) | data formatting | bytes 2752512 | tf_op jit(solution)/shard_map/transpose | solution.py:53
  256.9 6.5 %dot_general.15 = bf16[8,48,1792]{2,1,0:T(8,128)(2,1)} reshape(bf16[384,32,56]{2,1,0:T(8,128)(2,1)S(1)} %bitcast.30) | data formatting | bytes 2752512 | tf_op jit(solution)/shard_map/dot_general | solution.py:77
  263.4 3.9 %fusion = f32[8,48,864]{2,1,0:T(8,128)S(1)} fusion(bf16[8,48,1792]{2,1,0:T(8,128)(2,1)} %dot_general.15, bf16[864,1792]{1,0:T(8,128)(2,1)} %param.4), kind=kOutput, calls=%fused_computation | convolution fusion | flops 1189085184 | bytes 5799936 | tf_op jit(solution)/shard_map/dot_general | solution.py:77
  267.3 39.6 %all_to_all.10 = f32[8,48,864]{2,1,0:T(8,128)S(1)} all-to-all(f32[8,48,864]{2,1,0:T(8,128)S(1)} %fusion), channel_id=1, replica_groups=mesh['ckpt'=2,'row_0'=16,'row_1'=2,'col'=8] {'col'}, dimensions={0} | all-to-all | bytes 2654208 | tf_op jit(solution)/shard_map/all_to_all | solution.py:62
  306.9 0.7 reduce_sum.9
Async XLA Ops:
  8.3 21.9 %all-to-all-start = ((bf16[8,48,864]{2,1,0:T(8,128)(2,1)}), bf16[8,48,864]{2,1,0:T(8,128)(2,1)}, u32[]{:S(2)}, u32[]{:S(2)}) async-start(bf16[8,48,864]{2,1,0:T(8,128)(2,1)} %broadcast_in_dim.6), calls=%async_computation | async-start | bytes 1376256 | tf_op jit(solution)/shard_map/all_to_all | solution.py:20
  16.2 88.7 %reduce-scatter.3.cloned.1.call-start = ((), (), s32[]{:S(2)}) async-start(), calls=%async_computation.4 | async-start | bytes 9437184 | tf_op jit(solution)/shard_map/reduce_scatter | solution.py:32
  40.7 137.3 %reduce-scatter.5.cloned.1.call-start = ((), (), s32[]{:S(2)}) async-start(), calls=%async_computation.5 | async-start | bytes 3342336 | tf_op jit(solution)/shard_map/reduce_scatter | solution.py:32
  104.9 144.9 %all-gather.3.cloned.1.call-start = ((), (), s32[]{:S(2)}) async-start(), calls=%async_computation.6 | async-start | bytes 2064384 | tf_op jit(solution)/shard_map/all_gather | solution.py:49
Sparse Core Ops, SparseCore 0:
  40.9 63.9 reduce-scatter.2
  107.7 70.2 reduce-scatter.4
  211.4 38.4 all-gather.2
where the time goes:
time: 315 us; the launch traced here: 314 us
  waiting for transfers between devices  185 us (59%)
  blocking collectives  70.3 us (22%)
  local copies, waits for them, and re-layouts  26.9 us (9%)
  between operations  13.2 us (4%)
  matrix products  8.71 us (3%)
  starting transfers between devices  8.04 us (3%)
    reduce_scatter x2, waiting for transfers between devices, reduced_to_own(): blocks = lax.psum_scatter(blocks, axes[k], scatter_dimension=0, tiled=True)  137 us
    all_to_all x1, blocking collectives, summed_on_arrival(): blocks = lax.all_to_all(split_up(value, dim, count), axis, 0, 0, tiled=True)  39.6 us
    all_gather x1, waiting for transfers between devices, all_blocks(): blocks = lax.all_gather(blocks, axes[k], axis=0, tiled=True)  38.6 us
    all_gather x1, blocking collectives, all_blocks(): blocks = lax.all_gather(blocks, axes[k], axis=0, tiled=True)  30.7 us
    all_to_all x1, waiting for transfers between devices, copy_for_each(): return lax.all_to_all(copies, axis, split_axis=0, concat_axis=0, tiled=True)  9.44 us
    all_to_all x1, starting transfers between devices, copy_for_each(): return lax.all_to_all(copies, axis, split_axis=0, concat_axis=0, tiled=True)  7.86 us
    transpose x1, local copies, waits for them, and re-layouts, all_blocks(): blocks.transpose(*turned, *range(len(order), blocks.ndim))  7 us
    dot_general x1, local copies, waits for them, and re-layouts, on_device(): lax.dot_general(scaled, eigenbasis, (((1,), (1,)), ((), ())), preferred_e...  6.53 us
  transfers between devices with their start and end apart: 4, of which 4 were waited for; matrix products, arithmetic and copies ran while one was open for 1% of the time, Pallas kernels for 0%

commit v1 on v0

--- a/solution.py
+++ b/solution.py
@@ -46,7 +46,10 @@
 def all_blocks(value, axes, order):
     blocks = value[None]
     for k in order:
-        blocks = lax.all_gather(blocks, axes[k], axis=0, tiled=True)
+        size = lax.axis_size(axes[k])
+        tiles = jnp.stack([blocks for _ in range(size)])
+        tiles = lax.all_to_all(tiles, axes[k], split_axis=0, concat_axis=0)
+        blocks = jnp.concatenate(tiles, axis=0)
     carried = [lax.axis_size(axes[k]) for k in reversed(order)]
     blocks = blocks.reshape(*carried, *value.shape)
     turned = sorted(range(len(order)), key=lambda place: order[len(order) - 1 - place])

time: 315 us -> 298 us (0.946)
  waiting for transfers between devices: 185 us -> 147 us
  blocking collectives: 70.3 us -> 93.6 us
    all_to_all x0 -> x2, blocking collectives: none -> 51.3 us  [all_blocks(): tiles = lax.all_to_all(tiles, axes[k], split_axis=0, concat_axis=0)]
    all_gather x1 -> x0, waiting for transfers between devices: 38.6 us -> none  [all_blocks(): blocks = lax.all_gather(blocks, axes[k], axis=0, tiled=True)]
    all_gather x1 -> x0, blocking collectives: 30.7 us -> none  [all_blocks(): blocks = lax.all_gather(blocks, axes[k], axis=0, tiled=True)]
    transpose x1, local copies, waits for them, and re-layouts: 7 us -> 1.22 us  [all_blocks(): blocks.transpose(*turned, *range(len(order), blocks.ndim))]
    transpose x0 -> x1, local copies, waits for them, and re-layouts: none -> 5.34 us  [laid_out(): blocks = jnp.moveaxis(blocks, 0, dim)]
  transfers between devices with their start and end apart: 4 -> 3, of which waited for: 4 -> 3; matrix products, arithmetic and copies ran while one was open for 1% -> 2% of each run, Pallas kernels for 0% -> 0%
where the time goes in v1:
time: 298 us
  waiting for transfers between devices  147 us (49%)
  blocking collectives  93.6 us (31%)
  local copies, waits for them, and re-layouts  25.2 us (8%)
  between operations  13.5 us (5%)
  matrix products  8.7 us (3%)
  starting transfers between devices  7.98 us (3%)
    reduce_scatter x2, waiting for transfers between devices, reduced_to_own(): blocks = lax.psum_scatter(blocks, axes[k], scatter_dimension=0, tiled=True)  137 us
    all_to_all x2, blocking collectives, all_blocks(): tiles = lax.all_to_all(tiles, axes[k], split_axis=0, concat_axis=0)  51.3 us
    all_to_all x1, blocking collectives, summed_on_arrival(): blocks = lax.all_to_all(split_up(value, dim, count), axis, 0, 0, tiled=True)  42.3 us
    all_to_all x1, waiting for transfers between devices, copy_for_each(): return lax.all_to_all(copies, axis, split_axis=0, concat_axis=0, tiled=True)  9.44 us
    all_to_all x1, starting transfers between devices, copy_for_each(): return lax.all_to_all(copies, axis, split_axis=0, concat_axis=0, tiled=True)  7.86 us
    dot_general x1, local copies, waits for them, and re-layouts, on_device(): lax.dot_general(scaled, eigenbasis, (((1,), (1,)), ((), ())), preferred_e...  6.53 us
  transfers between devices with their start and end apart: 3, of which 3 were waited for; matrix products, arithmetic and copies ran while one was open for 2% of the time, Pallas kernels for 0%

profile of v1, /device:TPU:65, one launch (start us, length us, event | category | flops | bytes accessed | tf_op | source)
XLA Modules:
  0.0 297.7 jit_solution(16998039325422317722)
XLA Ops:
  6.5 1.8 broadcast_in_dim.3
  8.3 7.9 %all-to-all-start = ((bf16[8,48,864]{2,1,0:T(8,128)(2,1)}), bf16[8,48,864]{2,1,0:T(8,128)(2,1)}, u32[]{:S(2)}, u32[]{:S(2)}) async-start(bf16[8,48,864]{2,1,0:T(8,128)(2,1)} %broadcast_in_dim.3), calls=%async_computation | async-start | bytes 1376256 | tf_op jit(solution)/shard_map/all_to_all | solution.py:20
  16.2 0.1 reduce-scatter.3.cloned.1.call-start
  16.3 4.5 %copy.11 = bf16[864,1792]{0,1:T(8,128)(2,1)S(1)} copy(bf16[864,1792]{1,0:T(8,128)(2,1)} %param.4) | data formatting | bytes 6193152 | tf_op args[1]
  20.8 9.4 %all-to-all-done = bf16[8,48,864]{2,1,0:T(8,128)(2,1)} async-done(((bf16[8,48,864]{2,1,0:T(8,128)(2,1)}), bf16[8,48,864]{2,1,0:T(8,128)(2,1)}, u32[]{:S(2)}, u32[]{:S(2)}) %all-to-all-start) | async-done | bytes 663584 | tf_op jit(solution)/shard_map/all_to_all | solution.py:20
  30.2 4.8 %fusion.3 = f32[384,32,56]{0,2,1:T(8,128)} fusion(bf16[384,864,1]{1,0,2:T(8,128)(2,1)} %bitcast.1, bf16[32,56,864]{2,1,0:T(8,128)(2,1)S(1)} %bitcast.30), kind=kOutput, calls=%fused_computation.5 | convolution fusion | flops 1189085184 | bytes 6512640 | tf_op jit(solution)/shard_map/dot_general | solution.py:70
  35.0 5.6 %copy.13 = f32[2,16,384,56]{3,2,1,0:T(8,128)} copy(f32[2,16,384,56]{2,3,0,1:T(8,128)} %bitcast.31) | data formatting | bytes 5505024 | tf_op jit(solution)/shard_map/transpose | solution.py:30
  40.7 0.1 reduce-scatter.3.cloned.1.call-update
  40.7 0.1 reduce-scatter.5.cloned.1.call-start
  40.8 64.1 %reduce-scatter.3.cloned.1.call-done = f32[16,384,56]{2,1,0:T(8,128)} async-done(((f32[32,384,56]{2,1,0:T(8,128)}), f32[16,384,56]{2,1,0:T(8,128)}) %reduce-scatter.3.cloned.1.call-update) | async-done | bytes 1376272 | tf_op jit(solution)/shard_map/reduce_scatter | solution.py:32
  104.9 0.1 reduce-scatter.5.cloned.1.call-update
  104.9 73.1 %reduce-scatter.5.cloned.1.call-done = f32[1,384,56]{2,1,0:T(8,128)} async-done(((f32[16,384,56]{2,1,0:T(8,128)}), f32[1,384,56]{2,1,0:T(8,128)}) %reduce-scatter.5.cloned.1.call-update) | async-done | bytes 86032 | tf_op jit(solution)/shard_map/reduce_scatter | solution.py:32
  178.0 1.1 fusion.2
  179.1 0.1 copy.14
  179.2 0.1 stack.6
  179.3 32.5 %all_to_all.20 = bf16[16,1,384,56]{2,3,1,0:T(8,128)(2,1)S(1)} all-to-all(bf16[16,1,384,56]{2,3,1,0:T(8,128)(2,1)S(1)} %stack.6), channel_id=1, replica_groups=mesh['ckpt'=2,'row_0'=16,'row_1'=2,'col'=8] {'row_0'}, dimensions={0} | all-to-all | bytes 1376256 | tf_op jit(solution)/shard_map/all_to_all | solution.py:51
  211.8 0.2 pad_maximum_fusion
  212.0 18.8 %all_to_all.21 = bf16[2,16,384,56]{2,3,1,0:T(8,128)(2,1)S(1)} all-to-all(bf16[2,16,384,56]{2,3,1,0:T(8,128)(2,1)S(1)} %pad_maximum_fusion), channel_id=1, replica_groups=mesh['ckpt'=2,'row_0'=16,'row_1'=2,'col'=8] {'row_1'}, dimensions={0} | all-to-all | bytes 2752512 | tf_op jit(solution)/shard_map/all_to_all | solution.py:51
  230.8 1.2 copy.15
  232.0 5.3 %copy.16 = bf16[384,32,56]{2,1,0:T(8,128)(2,1)S(1)} copy(bf16[384,32,56]{0,2,1:T(8,128)(2,1)} %bitcast.29) | data formatting | bytes 2752512 | tf_op jit(solution)/shard_map/transpose | solution.py:13
  237.4 6.5 %dot_general.15 = bf16[8,48,1792]{2,1,0:T(8,128)(2,1)} reshape(bf16[384,32,56]{2,1,0:T(8,128)(2,1)S(1)} %copy.16) | data formatting | bytes 2752512 | tf_op jit(solution)/shard_map/dot_general | solution.py:80
  243.9 3.9 %fusion = f32[8,48,864]{2,1,0:T(8,128)S(1)} fusion(bf16[8,48,1792]{2,1,0:T(8,128)(2,1)} %dot_general.15, bf16[864,1792]{1,0:T(8,128)(2,1)} %param.4), kind=kOutput, calls=%fused_computation | convolution fusion | flops 1189085184 | bytes 5799936 | tf_op jit(solution)/shard_map/dot_general | solution.py:80
  247.8 42.3 %all_to_all.22 = f32[8,48,864]{2,1,0:T(8,128)S(1)} all-to-all(f32[8,48,864]{2,1,0:T(8,128)S(1)} %fusion), channel_id=1, replica_groups=mesh['ckpt'=2,'row_0'=16,'row_1'=2,'col'=8] {'col'}, dimensions={0} | all-to-all | bytes 2654208 | tf_op jit(solution)/shard_map/all_to_all | solution.py:65
  290.1 0.7 reduce_sum.9
Async XLA Ops:
  8.3 21.9 %all-to-all-start = ((bf16[8,48,864]{2,1,0:T(8,128)(2,1)}), bf16[8,48,864]{2,1,0:T(8,128)(2,1)}, u32[]{:S(2)}, u32[]{:S(2)}) async-start(bf16[8,48,864]{2,1,0:T(8,128)(2,1)} %broadcast_in_dim.3), calls=%async_computation | async-start | bytes 1376256 | tf_op jit(solution)/shard_map/all_to_all | solution.py:20
  16.2 88.7 %reduce-scatter.3.cloned.1.call-start = ((), (), s32[]{:S(2)}) async-start(), calls=%async_computation.6 | async-start | bytes 9437184 | tf_op jit(solution)/shard_map/reduce_scatter | solution.py:32
  40.7 137.3 %reduce-scatter.5.cloned.1.call-start = ((), (), s32[]{:S(2)}) async-start(), calls=%async_computation.7 | async-start | bytes 3342336 | tf_op jit(solution)/shard_map/reduce_scatter | solution.py:32
Sparse Core Ops, SparseCore 0:
  40.8 63.9 reduce-scatter.2
  107.7 70.2 reduce-scatter.4
